TPU v7x, 32 devices: a whole 2x2x4 slice. The times are simulated.
32 devices in a mesh: expert: 4 (over z), shard: 8 (over y, x, core).
Axes of the slice: x: 2, y: 2, z: 4, core: 2. Of those that a mesh axis runs over, the one named last changes fastest.
Arguments:
- master_down: float32 [16, 6400, 4096], P('expert', None, 'shard'), may hold values from -0.109375 to 0.109375
- second_down: bfloat16 [16, 6400, 4096], P('expert', None, 'shard'), may hold values from -0.0390625 to 0.0390625
- router_weight: float32 [4096, 16], P('shard', 'expert'), may hold values from -0.09375 to 0.09375
- router_gain: float32 [4096], P('shard'), may hold values from 0.25 to 1.75
Outputs:
- final_down: bfloat16 [16, 6400, 4096], P('expert', 'shard')
- scale_down: float32 [16, 6400], P('expert', 'shard')
- serve_router: bfloat16 [4096, 16], replicated
All inputs are finite; a program needn't handle non-finite values.
Results may differ from a plain program's by a relative error of at most 0.001.
Values may be sent and summed in bfloat16 or wider, within the bound.
A program may use at most 256 MiB of HBM per device.

v0:
```python
import functools

import jax
import jax.numpy as jnp
from jax import lax
from jax.experimental import pallas as pl
from jax.experimental.pallas import tpu as pltpu
from jax.sharding import PartitionSpec as P

MESH = pl.DeviceIdType.MESH
QUEUE = 3
READS = 3
SKEW = 1


def rows_per_chunk(rows):
    return max(r for r in range(16, 129, 16) if rows % r == 0)


def flipped(index, mask):
    out, bit = 0, 1
    while bit <= mask:
        own = lax.rem(index // bit, 2)
        if mask & bit:
            out = out + bit * (1 - 2 * own)
        bit *= 2
    return index + out


def kernel(
    shards, groups, master, second, weight, gain,
    final, scale, router,
    sum_master, sum_second, norm_master, norm_second, ready,
    part, landed, rpart, rall,
    sum_sems, norm_sems, send_sems, own_sems, final_sems,
    part_send, part_recv, rsend, rrecv, gsend, grecv,
    weight_here, gain_here, small_sems,
):
    experts, _, rows, cols = master.shape
    take = rows_per_chunk(rows)
    blocks = rows // take
    chunks = experts * blocks
    stages = shards.bit_length() - 1
    me = lax.axis_index("shard")
    group = lax.axis_index("expert")
    lag = SKEW * stages

    def reads(k, bufs, sems):
        slot = lax.rem(k, READS)
        e, b = k // blocks, lax.rem(k, blocks)
        where = pl.ds(pl.multiple_of(b * take, 16), take)
        return [
            pltpu.make_async_copy(src.at[e, :, where, :], buf.at[slot], sems.at[i, slot])
            for i, (src, buf) in enumerate(zip((master, second), bufs))
        ]

    sum_bufs, norm_bufs = (sum_master, sum_second), (norm_master, norm_second)

    for k in range(min(READS, chunks)):
        for c in reads(k, sum_bufs, sum_sems):
            c.start()

    small = [
        pltpu.make_async_copy(weight, weight_here, small_sems.at[0]),
        pltpu.make_async_copy(gain, gain_here, small_sems.at[1]),
    ]
    for c in small:
        c.start()
    barrier = pltpu.get_barrier_semaphore()
    for o in range(1, shards):
        pl.semaphore_signal(barrier, inc=1, device_id={"shard": flipped(me, o)}, device_id_type=MESH)
    for o in range(1, groups):
        pl.semaphore_signal(barrier, inc=1, device_id={"expert": lax.rem(group + o, groups)}, device_id_type=MESH)

    for c in small:
        c.wait()
    product = (weight_here[...] * gain_here[...]).astype(jnp.bfloat16)
    rpart[...] = product
    mine = pl.ds(pl.multiple_of(me * cols, 128), cols)
    rall[group, :, mine] = product
    for k in range(min(READS, chunks)):
        for c in reads(k, norm_bufs, norm_sems):
            c.start()
    pl.semaphore_wait(barrier, shards + groups - 2)

    def exchange(stage, k):
        return pltpu.make_async_remote_copy(
            src_ref=part.at[stage, k],
            dst_ref=landed.at[stage, k],
            send_sem=part_send.at[stage],
            recv_sem=part_recv.at[stage, k],
            device_id={"shard": flipped(me, 1 << stage)},
            device_id_type=MESH,
        )

    eye = lax.broadcasted_iota(jnp.int32, (take, 128), 0) == lax.broadcasted_iota(jnp.int32, (take, 128), 1)

    def send(k, o):
        slot = lax.rem(k, QUEUE)
        e, b = k // blocks, lax.rem(k, blocks)
        where = pl.ds(pl.multiple_of(b * take, 16), take)
        to = flipped(me, o)
        return pltpu.make_async_remote_copy(
            src_ref=ready.at[slot, to],
            dst_ref=final.at[e, where, mine],
            send_sem=send_sems.at[slot],
            recv_sem=final_sems.at[me],
            device_id={"shard": to},
            device_id_type=MESH,
        )

    def keep(k):
        slot = lax.rem(k, QUEUE)
        e, b = k // blocks, lax.rem(k, blocks)
        where = pl.ds(pl.multiple_of(b * take, 16), take)
        return pltpu.make_async_copy(ready.at[slot, me], final.at[e, where, mine], own_sems.at[slot])

    def drain(k):
        slot = lax.rem(k, QUEUE)
        several = ready.at[slot, pl.ds(0, shards - 1)]
        pltpu.make_async_copy(several, several, send_sems.at[slot]).wait()
        keep(k).wait()

    def tick(t, carry):
        @pl.when(t < chunks)
        def _():
            slot = lax.rem(t, READS)
            for c in reads(t, sum_bufs, sum_sems):
                c.wait()

            def one(d, carry):
                x = sum_master[slot, d] + sum_second[slot, d].astype(jnp.float32)
                column = jnp.sum(x * x, axis=1, keepdims=True)
                part[0, t, pl.ds(d, 1), :] = jnp.sum(jnp.where(eye, column, 0.0), axis=0, keepdims=True)
                return carry

            lax.fori_loop(0, shards, one, 0, unroll=2)

            @pl.when(t + READS < chunks)
            def _():
                for c in reads(t + READS, sum_bufs, sum_sems):
                    c.start()

        for stage in range(1, stages):
            k = t - SKEW * stage

            @pl.when((k >= 0) & (k < chunks))
            def _():
                exchange(stage - 1, k).wait_recv()
                part[stage, k] = part[stage - 1, k] + landed[stage - 1, k]

        for stage in range(stages):
            k = t - SKEW * stage

            @pl.when((k >= 0) & (k < chunks))
            def _():
                exchange(stage, k).start()

        k = t - lag

        @pl.when((k >= 0) & (k < chunks))
        def _():
            slot = lax.rem(k, READS)
            out = lax.rem(k, QUEUE)
            exchange(stages - 1, k).wait_recv()
            part[stages, k] = jnp.sqrt(part[stages - 1, k] + landed[stages - 1, k])
            scale[pl.ds(k, 1), :] = part[stages, k, pl.ds(me, 1), :]
            for c in reads(k, norm_bufs, norm_sems):
                c.wait()

            @pl.when(k >= QUEUE)
            def _():
                drain(k - QUEUE)

            def one(d, carry):
                row = 1.0 / part[stages, k, pl.ds(d, 1), :]
                column = jnp.sum(jnp.where(eye, row, 0.0), axis=1, keepdims=True)
                x = norm_master[slot, d] + norm_second[slot, d].astype(jnp.float32)
                ready[out, d] = (x * column).astype(jnp.bfloat16)
                return carry

            lax.fori_loop(0, shards, one, 0, unroll=2)

            @pl.when(k + READS < chunks)
            def _():
                for c in reads(k + READS, norm_bufs, norm_sems):
                    c.start()

            for o in range(shards - 1, 0, -1):
                send(k, o).start()
            keep(k).start()

        return carry

    def rows_copy(o):
        return pltpu.make_async_remote_copy(
            src_ref=rpart,
            dst_ref=rall.at[group, :, mine],
            send_sem=rsend,
            recv_sem=rrecv.at[me],
            device_id={"shard": flipped(me, o)},
            device_id_type=MESH,
        )

    for o in range(1, shards):
        rows_copy(o).start()

    lax.fori_loop(0, chunks + lag, tick, 0)

    def group_copy(o):
        return pltpu.make_async_remote_copy(
            src_ref=rall.at[group],
            dst_ref=rall.at[group],
            send_sem=gsend.at[o],
            recv_sem=grecv.at[group],
            device_id={"expert": lax.rem(group + o, groups)},
            device_id_type=MESH,
        )

    for o in range(1, shards):
        rows_copy(o).wait_send()
        other = flipped(me, o)
        there = rall.at[group, :, pl.ds(pl.multiple_of(other * cols, 128), cols)]
        pltpu.make_async_copy(there, there, rrecv.at[other]).wait()
    for o in range(1, groups):
        group_copy(o).start()
    for o in range(1, groups):
        other = lax.rem(group + o, groups)
        pltpu.make_async_copy(rall.at[other], rall.at[other], grecv.at[other]).wait()
        group_copy(o).wait_send()
    router[...] = rall[...]

    for stage in range(stages):
        pltpu.make_async_copy(part.at[stage], part.at[stage], part_send.at[stage]).wait()
    for k in range(max(0, chunks - QUEUE), chunks):
        drain(k)
    for o in range(1, shards):
        other = flipped(me, o)
        there = final.at[:, :, pl.ds(pl.multiple_of(other * cols, 128), cols)]
        pltpu.make_async_copy(there, there, final_sems.at[other]).wait()


def local(shards, groups, master_down, second_down, router_weight, router_gain):
    experts, d_expert, cols = master_down.shape
    rows = d_expert // shards
    take = rows_per_chunk(rows)
    chunks = experts * (rows // take)
    stages = shards.bit_length() - 1
    gcols = router_weight.shape[1]
    f32, bf16 = jnp.float32, jnp.bfloat16
    final, scale, router = pl.pallas_call(
        functools.partial(kernel, shards, groups),
        out_shape=(
            jax.ShapeDtypeStruct((experts, rows, cols * shards), bf16),
            jax.ShapeDtypeStruct((chunks, 128), f32),
            jax.ShapeDtypeStruct((groups, gcols, cols * shards), bf16),
        ),
        in_specs=[pl.BlockSpec(memory_space=pl.ANY)] * 2 + [pl.BlockSpec(memory_space=pltpu.HBM)] * 2,
        out_specs=(
            pl.BlockSpec(memory_space=pl.ANY),
            pl.BlockSpec(memory_space=pltpu.VMEM),
            pl.BlockSpec(memory_space=pltpu.VMEM),
        ),
        scratch_shapes=[
            pltpu.VMEM((READS, shards, take, cols), f32),
            pltpu.VMEM((READS, shards, take, cols), bf16),
            pltpu.VMEM((READS, shards, take, cols), f32),
            pltpu.VMEM((READS, shards, take, cols), bf16),
            pltpu.VMEM((QUEUE, shards, take, cols), bf16),
            pltpu.VMEM((stages + 1, chunks, shards, 128), f32),
            pltpu.VMEM((stages, chunks, shards, 128), f32),
            pltpu.VMEM((gcols, cols), bf16),
            pltpu.VMEM((groups, gcols, cols * shards), bf16),
            pltpu.SemaphoreType.DMA((2, READS)),
            pltpu.SemaphoreType.DMA((2, READS)),
            pltpu.SemaphoreType.DMA((QUEUE,)),
            pltpu.SemaphoreType.DMA((QUEUE,)),
            pltpu.SemaphoreType.DMA((shards,)),
            pltpu.SemaphoreType.DMA((stages,)),
            pltpu.SemaphoreType.DMA((stages, chunks)),
            pltpu.SemaphoreType.DMA,
            pltpu.SemaphoreType.DMA((shards,)),
            pltpu.SemaphoreType.DMA((groups,)),
            pltpu.SemaphoreType.DMA((groups,)),
            pltpu.VMEM((gcols, cols), f32),
            pltpu.VMEM((1, cols), f32),
            pltpu.SemaphoreType.DMA((2,)),
        ],
        compiler_params=pltpu.CompilerParams(collective_id=0, has_side_effects=True, vmem_limit_bytes=32 * 2**20),
    )(
        master_down.reshape(experts, shards, rows, cols),
        second_down.reshape(experts, shards, rows, cols),
        router_weight.T,
        router_gain[None, :],
    )
    scale = scale[:, :take].reshape(experts, rows)
    return (final, scale, router.reshape(groups * gcols, cols * shards).T)


def solution(mesh):
    shards, groups = mesh.shape["shard"], mesh.shape["expert"]
    return jax.shard_map(
        functools.partial(local, shards, groups),
        mesh=mesh,
        in_specs=(
            P("expert", None, "shard"),
            P("expert", None, "shard"),
            P("shard", "expert"),
            P("shard"),
        ),
        out_specs=(P("expert", "shard", None), P("expert", "shard"), P()),
        check_vma=False,
    )
```

profile of v0, /device:TPU:0, one launch (start us, length us, event | category | flops | bytes accessed | tf_op | source)
XLA Modules:
  0.0 320.6 jit_solution(17256772812710226369)
XLA Ops:
  0.6 0.0 copy-start
  0.6 0.7 copy-done
  1.3 0.0 copy-start.1
  1.3 0.7 copy-done.1
  2.0 299.3 %shard_map.67 = (bf16[4,800,4096]{2,1,0:T(8,128)(2,1)}, f32[40,128]{1,0:T(8,128)S(1)}, bf16[4,4,4096]{2,1,0:T(4,128)(2,1)S(1)}) custom-call(f32[4,8,800,512]{3,2,1,0:T(8,128)} %bitcast.9, bf16[4,8,800,512]{3,2,1,0:T(8,128)(2,1)} %bitcast.10, f32[4,512]{1,0:T(4,128)S(1)} %bitcast.7, f32[1,512]{1,0:T(1,128)S(1)} %bitcast.8), custom_call_target="tpu_custom_call" | custom-call | tf_op jit(solution)/shard_map/pallas_call | solution.py:251
  301.3 0.7 reshape.20
  302.0 0.7 reshape.21
  302.7 17.9 %copy.8 = bf16[4,800,4096]{2,1,0:T(8,128)(2,1)} copy(bf16[4,800,4096]{2,1,0:T(8,128)(2,1)} %get-tuple-element.12) | data formatting | bytes 52428800
Async XLA Ops:
  0.6 0.7 copy-start
  1.3 0.7 copy-start.1
where the time goes:
time: 321 us
  Pallas kernels  299 us (93%)
  local copies, waits for them, and re-layouts  20.7 us (6%)
    pallas_call x1, Pallas kernels, local(): pl.pallas_call(functools.partial(kernel, shards, groups), out_shape=(jax....  299 us
    unnamed x5, local copies, waits for them, and re-layouts  19.3 us

commit v1 on v0

v1 whole, which is shorter than its diff:
```python
import functools

import jax
import jax.numpy as jnp
from jax import lax
from jax.experimental import pallas as pl
from jax.experimental.pallas import tpu as pltpu
from jax.sharding import PartitionSpec as P

MESH = pl.DeviceIdType.MESH
QUEUE = 3
READS = 3
DIRECT = 2
GROUP = 16
LANES = 128


def rows_per_chunk(rows):
    return max(r for r in range(16, 129, 16) if rows % r == 0)


def flipped(index, mask):
    out, bit = 0, 1
    while bit <= mask:
        own = lax.rem(index // bit, 2)
        if mask & bit:
            out = out + bit * (1 - 2 * own)
        bit *= 2
    return index + out


def kernel(
    shards, groups, master, second, weight, gain,
    final, scale, router,
    sum_master, sum_second, norm_master, norm_second, ready,
    part, landed, total, early, rpart, rall,
    sum_sems, norm_sems, send_sems, own_sems, final_sems,
    part_send, part_recv, total_send, total_recv, early_send, early_recv,
    rsend, rrecv, gsend, grecv, weight_here, gain_here, small_sems, own,
):
    experts, _, rows, cols = master.shape
    take = rows_per_chunk(rows)
    blocks = rows // take
    chunks = experts * blocks
    bits = shards.bit_length() - 1
    lag = bits + 1
    per = LANES // GROUP
    parts = take // GROUP
    lines = shards * take // LANES
    me = lax.axis_index("shard")
    group = lax.axis_index("expert")
    parity = lax.rem(me, 2)

    barrier = pltpu.get_barrier_semaphore()
    for o in range(shards - 1, 0, -1):
        pl.semaphore_signal(barrier, inc=1, device_id={"shard": flipped(me, o)}, device_id_type=MESH)
    for o in range(1, groups):
        pl.semaphore_signal(barrier, inc=1, device_id={"expert": lax.rem(group + o, groups)}, device_id_type=MESH)

    def reads(k, bufs, sems):
        slot = lax.rem(k, READS)
        e, b = k // blocks, lax.rem(k, blocks)
        where = pl.ds(pl.multiple_of(b * take, 16), take)
        return [
            pltpu.make_async_copy(src.at[e, :, where, :], buf.at[slot], sems.at[i, slot])
            for i, (src, buf) in enumerate(zip((master, second), bufs))
        ]

    sum_bufs, norm_bufs = (sum_master, sum_second), (norm_master, norm_second)

    for k in range(min(READS, chunks)):
        for c in reads(k, sum_bufs, sum_sems):
            c.start()
    small = [
        pltpu.make_async_copy(weight, weight_here, small_sems.at[0]),
        pltpu.make_async_copy(gain, gain_here, small_sems.at[1]),
    ]
    for c in small:
        c.start()
    for k in range(min(READS, chunks)):
        for c in reads(k, norm_bufs, norm_sems):
            c.start()

    mine = pl.ds(pl.multiple_of(me * cols, 128), cols)

    shift = lax.broadcasted_iota(jnp.int32, (GROUP, LANES), 1) - lax.broadcasted_iota(jnp.int32, (GROUP, LANES), 0)

    def place(j):
        d, i = j // parts, lax.rem(j, parts)
        return d, pl.ds(pl.multiple_of(i * GROUP, GROUP), GROUP)

    def row_sums(k, dst):
        slot = lax.rem(k, READS)
        for c in reads(k, sum_bufs, sum_sems):
            c.wait()

        def one(s, carry):
            acc = jnp.zeros((GROUP, LANES), jnp.float32)
            for m in range(per):
                d, where = place(s * per + m)
                x = sum_master[slot, d, where, :] + sum_second[slot, d, where, :].astype(jnp.float32)
                column = jnp.sum(x * x, axis=1, keepdims=True)
                acc = acc + jnp.where(shift == GROUP * m, column, 0.0)
            dst[s] = jnp.sum(acc, axis=0, keepdims=True)
            return carry

        lax.fori_loop(0, lines, one, 0)

        @pl.when(k + READS < chunks)
        def _():
            for c in reads(k + READS, sum_bufs, sum_sems):
                c.start()

    def early_copy(k, o):
        return pltpu.make_async_remote_copy(
            src_ref=early.at[k, me],
            dst_ref=early.at[k, me],
            send_sem=early_send.at[k],
            recv_sem=early_recv.at[k, me],
            device_id={"shard": flipped(me, o)},
            device_id_type=MESH,
        )

    def exchange(stage, k):
        return pltpu.make_async_remote_copy(
            src_ref=part.at[stage, k],
            dst_ref=landed.at[stage, k],
            send_sem=part_send.at[stage],
            recv_sem=part_recv.at[stage, k],
            device_id={"shard": flipped(me, 1 << stage)},
            device_id_type=MESH,
        )

    def hand_over(k):
        return pltpu.make_async_remote_copy(
            src_ref=total.at[k],
            dst_ref=total.at[k],
            send_sem=total_send,
            recv_sem=total_recv.at[k],
            device_id={"shard": flipped(me, 1)},
            device_id_type=MESH,
        )

    def send(k, o):
        slot = lax.rem(k, QUEUE)
        e, b = k // blocks, lax.rem(k, blocks)
        where = pl.ds(pl.multiple_of(b * take, 16), take)
        to = flipped(me, o)
        return pltpu.make_async_remote_copy(
            src_ref=ready.at[slot, to],
            dst_ref=final.at[e, where, mine],
            send_sem=send_sems.at[slot],
            recv_sem=final_sems.at[me],
            device_id={"shard": to},
            device_id_type=MESH,
        )

    def keep(k):
        slot = lax.rem(k, QUEUE)
        e, b = k // blocks, lax.rem(k, blocks)
        where = pl.ds(pl.multiple_of(b * take, 16), take)
        return pltpu.make_async_copy(ready.at[slot, me], final.at[e, where, mine], own_sems.at[slot])

    def drain(k):
        slot = lax.rem(k, QUEUE)
        several = ready.at[slot, pl.ds(0, shards - 1)]
        pltpu.make_async_copy(several, several, send_sems.at[slot]).wait()
        keep(k).wait()

    def normalise(k):
        slot = lax.rem(k, READS)
        out = lax.rem(k, QUEUE)
        for c in reads(k, norm_bufs, norm_sems):
            c.wait()

        @pl.when(k >= QUEUE)
        def _():
            drain(k - QUEUE)

        def one(s, carry):
            line = 1.0 / jnp.sqrt(total[k, s])
            for m in range(per):
                d, where = place(s * per + m)
                column = jnp.sum(jnp.where(shift == GROUP * m, line, 0.0), axis=1, keepdims=True)
                x = norm_master[slot, d, where, :] + norm_second[slot, d, where, :].astype(jnp.float32)
                ready[out, d, where, :] = (x * column).astype(jnp.bfloat16)
            return carry

        lax.fori_loop(0, lines, one, 0)

        @pl.when(k + READS < chunks)
        def _():
            for c in reads(k + READS, norm_bufs, norm_sems):
                c.start()

        for o in range(shards - 1, 0, -1):
            send(k, o).start()
        keep(k).start()

    first = min(DIRECT, chunks)
    row_sums(0, early.at[0, me])
    pl.semaphore_wait(barrier, shards + groups - 2)
    for k in range(first):
        if k:
            row_sums(k, early.at[k, me])
        for o in range(shards - 1, 0, -1):
            early_copy(k, o).start()

    for c in small:
        c.wait()
    product = (weight_here[...] * gain_here[...]).astype(jnp.bfloat16)
    rpart[...] = product
    rall[group, :, mine] = product

    def rows_copy(o):
        return pltpu.make_async_remote_copy(
            src_ref=rpart,
            dst_ref=rall.at[group, :, mine],
            send_sem=rsend,
            recv_sem=rrecv.at[me],
            device_id={"shard": flipped(me, o)},
            device_id_type=MESH,
        )

    for o in range(1, shards):
        rows_copy(o).start()

    def tick(t, carry):
        @pl.when(t < chunks)
        def _():
            row_sums(t, part.at[0, t])

            @pl.when(lax.rem(t, 2) != parity)
            def _():
                exchange(0, t).start()

        n = t - lag

        @pl.when((n >= 0) & (n < first))
        def _():
            for o in range(1, shards):
                other = flipped(me, o)
                pltpu.make_async_copy(early.at[n, other], early.at[n, other], early_recv.at[n, other]).wait()
            sums = early[n, 0]
            for s in range(1, shards):
                sums = sums + early[n, s]
            total[n] = sums

        @pl.when((n >= first) & (lax.rem(n, 2) != parity))
        def _():
            hand_over(n).wait_recv()

        @pl.when(n >= 0)
        def _():
            normalise(n)

        for stage in range(bits):
            k = t - 1 - stage

            @pl.when((k >= first) & (k < chunks) & (lax.rem(k, 2) == parity))
            def _():
                exchange(stage, k).wait_recv()
                if stage + 1 < bits:
                    part[stage + 1, k] = part[stage, k] + landed[stage, k]
                    exchange(stage + 1, k).start()
                else:
                    total[k] = part[stage, k] + landed[stage, k]
                    hand_over(k).start()

        return carry

    lax.fori_loop(first, chunks + lag, tick, 0)

    def group_copy(o):
        return pltpu.make_async_remote_copy(
            src_ref=rall.at[group],
            dst_ref=rall.at[group],
            send_sem=gsend.at[o],
            recv_sem=grecv.at[group],
            device_id={"expert": lax.rem(group + o, groups)},
            device_id_type=MESH,
        )

    for o in range(1, shards):
        rows_copy(o).wait_send()
        other = flipped(me, o)
        there = rall.at[group, :, pl.ds(pl.multiple_of(other * cols, 128), cols)]
        pltpu.make_async_copy(there, there, rrecv.at[other]).wait()
    for o in range(1, groups):
        group_copy(o).start()

    here = rows // GROUP

    def own_lines(e, carry):
        for line in range(-(-here // per)):
            acc = jnp.zeros((GROUP, LANES), jnp.float32)
            for m in range(min(per, here - line * per)):
                b, i = divmod(line * per + m, parts)
                j = me * parts + i
                source = total[e * blocks + b, j // per]
                column = jnp.sum(jnp.where(shift == GROUP * lax.rem(j, per), source, 0.0), axis=1, keepdims=True)
                acc = acc + jnp.where(shift == GROUP * m, column, 0.0)
            own[e, :, line * LANES : (line + 1) * LANES] = jnp.sqrt(jnp.sum(acc, axis=0, keepdims=True))
        return carry

    lax.fori_loop(0, experts, own_lines, 0)
    for e in range(experts):
        scale[e : e + 1, :] = own[e, :, :rows]

    for o in range(1, groups):
        other = lax.rem(group + o, groups)
        pltpu.make_async_copy(rall.at[other], rall.at[other], grecv.at[other]).wait()
        group_copy(o).wait_send()
    gcols = weight.shape[0]
    spot = lax.broadcasted_iota(jnp.int32, router.shape, 0)
    table = jnp.zeros(router.shape, jnp.float32)
    for g in range(groups):
        block = rall[g].astype(jnp.float32)
        for c in range(gcols):
            table = jnp.where(spot == g * gcols + c, block[c : c + 1, :], table)
    router[...] = table.astype(jnp.bfloat16)

    for k in range(first):
        several = early.at[k, pl.ds(0, shards - 1)]
        pltpu.make_async_copy(several, several, early_send.at[k]).wait()

    def settle(k, carry):
        @pl.when(lax.rem(k, 2) != parity)
        def _():
            exchange(0, k).wait_send()

        @pl.when(lax.rem(k, 2) == parity)
        def _():
            for stage in range(1, bits):
                exchange(stage, k).wait_send()
            hand_over(k).wait_send()

        return carry

    lax.fori_loop(first, chunks, settle, 0)
    for k in range(max(0, chunks - QUEUE), chunks):
        drain(k)
    for o in range(1, shards):
        other = flipped(me, o)
        there = final.at[:, :, pl.ds(pl.multiple_of(other * cols, 128), cols)]
        pltpu.make_async_copy(there, there, final_sems.at[other]).wait()


def write_out(final, scale, router, final_out, scale_out, router_out, sems):
    experts = final.shape[0]
    copies = [
        pltpu.make_async_copy(scale, scale_out, sems.at[experts]),
        pltpu.make_async_copy(router, router_out, sems.at[experts + 1]),
    ]
    copies += [pltpu.make_async_copy(final.at[e], final_out.at[e], sems.at[e]) for e in range(experts)]
    for c in copies:
        c.start()
    for c in copies:
        c.wait()


def local(shards, groups, master_down, second_down, router_weight, router_gain):
    experts, d_expert, cols = master_down.shape
    rows = d_expert // shards
    take = rows_per_chunk(rows)
    chunks = experts * (rows // take)
    bits = shards.bit_length() - 1
    lines = shards * take // LANES
    gcols = router_weight.shape[1]
    f32, bf16 = jnp.float32, jnp.bfloat16
    first = min(DIRECT, chunks)
    shapes = (
        jax.ShapeDtypeStruct((experts, rows, cols * shards), bf16),
        jax.ShapeDtypeStruct((experts, rows), f32),
        jax.ShapeDtypeStruct((groups * gcols, cols * shards), bf16),
    )
    in_vmem = pl.BlockSpec(memory_space=pltpu.VMEM)
    in_hbm = pl.BlockSpec(memory_space=pltpu.HBM)
    anywhere = pl.BlockSpec(memory_space=pl.ANY)
    dma = pltpu.SemaphoreType.DMA
    inside = pl.pallas_call(
        functools.partial(kernel, shards, groups),
        out_shape=shapes,
        in_specs=[anywhere] * 2 + [in_hbm] * 2,
        out_specs=(in_vmem,) * 3,
        scratch_shapes=[
            pltpu.VMEM((READS, shards, take, cols), f32),
            pltpu.VMEM((READS, shards, take, cols), bf16),
            pltpu.VMEM((READS, shards, take, cols), f32),
            pltpu.VMEM((READS, shards, take, cols), bf16),
            pltpu.VMEM((QUEUE, shards, take, cols), bf16),
            pltpu.VMEM((bits, chunks, lines, 1, LANES), f32),
            pltpu.VMEM((bits, chunks, lines, 1, LANES), f32),
            pltpu.VMEM((chunks, lines, 1, LANES), f32),
            pltpu.VMEM((first, shards, lines, 1, LANES), f32),
            pltpu.VMEM((gcols, cols), bf16),
            pltpu.VMEM((groups, gcols, cols * shards), bf16),
            dma((2, READS)),
            dma((2, READS)),
            dma((QUEUE,)),
            dma((QUEUE,)),
            dma((shards,)),
            dma((bits,)),
            dma((bits, chunks)),
            dma,
            dma((chunks,)),
            dma((first,)),
            dma((first, shards)),
            dma,
            dma((shards,)),
            dma((groups,)),
            dma((groups,)),
            pltpu.VMEM((gcols, cols), f32),
            pltpu.VMEM((1, cols), f32),
            dma((2,)),
            pltpu.VMEM((experts, 1, -(-rows // LANES) * LANES), f32),
        ],
        compiler_params=pltpu.CompilerParams(collective_id=0, has_side_effects=True, vmem_limit_bytes=28 * 2**20),
    )(
        master_down.reshape(experts, shards, rows, cols),
        second_down.reshape(experts, shards, rows, cols),
        pltpu.with_memory_space_constraint(router_weight.T, pltpu.HBM),
        pltpu.with_memory_space_constraint(router_gain[None, :], pltpu.HBM),
    )
    final, scale, router = pl.pallas_call(
        write_out,
        out_shape=shapes,
        in_specs=[in_vmem] * 3,
        out_specs=(in_hbm,) * 3,
        scratch_shapes=[dma((experts + 2,))],
        compiler_params=pltpu.CompilerParams(vmem_limit_bytes=2**20),
    )(*inside)
    return (final, scale, router.T)


def solution(mesh):
    shards, groups = mesh.shape["shard"], mesh.shape["expert"]
    return jax.shard_map(
        functools.partial(local, shards, groups),
        mesh=mesh,
        in_specs=(
            P("expert", None, "shard"),
            P("expert", None, "shard"),
            P("shard", "expert"),
            P("shard"),
        ),
        out_specs=(P("expert", "shard", None), P("expert", "shard"), P()),
        check_vma=False,
    )
```

time: 321 us -> 307 us (0.956)
  local copies, waits for them, and re-layouts: 20.7 us -> 0 us
  Pallas kernels: 299 us -> 306 us
    unnamed x5 -> x0, local copies, waits for them, and re-layouts: 19.3 us -> none
    pallas_call x1 -> x2, Pallas kernels: 299 us -> 306 us  [the longest x1 297 us: local(): pl.pallas_call(functools.partial(kernel, shards, groups), out_shape=shape...]
where the time goes in v1:
time: 307 us
  Pallas kernels  306 us (100%)
    pallas_call x1, Pallas kernels, local(): pl.pallas_call(functools.partial(kernel, shards, groups), out_shape=shape...  297 us
    pallas_call x1, Pallas kernels, local(): pl.pallas_call(write_out, out_shape=shapes, in_specs=[in_vmem] * 3, out_s...  8.99 us

profile of v1, /device:TPU:0, one launch (start us, length us, event | category | flops | bytes accessed | tf_op | source)
XLA Modules:
  0.0 306.6 jit_solution(10411135236575718155)
XLA Ops:
  0.6 297.0 %shard_map.67 = (bf16[4,800,4096]{2,1,0:T(8,128)(2,1)S(1)}, f32[4,800]{1,0:T(4,128)S(1)}, bf16[16,4096]{1,0:T(8,128)(2,1)S(1)}) custom-call(f32[4,8,800,512]{3,2,1,0:T(8,128)} %bitcast.5, bf16[4,8,800,512]{3,2,1,0:T(8,128)(2,1)} %bitcast.6, f32[4,512]{1,0:T(4,128)} %bitcast.7, f32[1,512]{1,0:T(1,128)} %bitcast.8), custom_call_target="tpu_custom_call" | custom-call | tf_op jit(solution)/shard_map/pallas_call | solution.py:381
  297.6 9.0 %shard_map.68 = (bf16[4,800,4096]{2,1,0:T(8,128)(2,1)}, f32[4,800]{1,0:T(4,128)}, bf16[16,4096]{1,0:T(8,128)(2,1)}) custom-call(bf16[4,800,4096]{2,1,0:T(8,128)(2,1)S(1)} %get-tuple-element.9.final, f32[4,800]{1,0:T(4,128)S(1)} %get-tuple-element.10.scale, bf16[16,4096]{1,0:T(8,128)(2,1)S(1)} %get-tuple-element.11.router), custom_call_target="tpu_custom_call" | custom-call | tf_op jit(solution)/shard_map/pallas_call | solution.py:425

commit v2 on v1

--- a/solution.py
+++ b/solution.py
@@ -11,6 +11,7 @@
 QUEUE = 3
 READS = 3
 DIRECT = 2
+RING = 8
 GROUP = 16
 LANES = 128
 
@@ -29,6 +30,15 @@
     return index + out
 
 
+def crossed(index, mask, bits):
+    out, bit = 0, 1
+    for _ in range(bits):
+        a, b = lax.rem(index // bit, 2), lax.rem(mask // bit, 2)
+        out = out + bit * (a + b - 2 * a * b)
+        bit *= 2
+    return out
+
+
 def kernel(
     shards, groups, master, second, weight, gain,
     final, scale, router,
@@ -36,7 +46,7 @@
     part, landed, total, early, rpart, rall,
     sum_sems, norm_sems, send_sems, own_sems, final_sems,
     part_send, part_recv, total_send, total_recv, early_send, early_recv,
-    rsend, rrecv, gsend, grecv, weight_here, gain_here, small_sems, own,
+    rsend, rrecv, gsend, grecv, weight_here, gain_here, small_sems, own, inverse,
 ):
     experts, _, rows, cols = master.shape
     take = rows_per_chunk(rows)
@@ -116,7 +126,7 @@
             src_ref=early.at[k, me],
             dst_ref=early.at[k, me],
             send_sem=early_send.at[k],
-            recv_sem=early_recv.at[k, me],
+            recv_sem=early_recv.at[k],
             device_id={"shard": flipped(me, o)},
             device_id_type=MESH,
         )
@@ -126,7 +136,7 @@
             src_ref=part.at[stage, k],
             dst_ref=landed.at[stage, k],
             send_sem=part_send.at[stage],
-            recv_sem=part_recv.at[stage, k],
+            recv_sem=part_recv.at[stage, lax.rem(k, RING)],
             device_id={"shard": flipped(me, 1 << stage)},
             device_id_type=MESH,
         )
@@ -136,16 +146,15 @@
             src_ref=total.at[k],
             dst_ref=total.at[k],
             send_sem=total_send,
-            recv_sem=total_recv.at[k],
+            recv_sem=total_recv.at[lax.rem(k, RING)],
             device_id={"shard": flipped(me, 1)},
             device_id_type=MESH,
         )
 
-    def send(k, o):
+    def send(k, to):
         slot = lax.rem(k, QUEUE)
         e, b = k // blocks, lax.rem(k, blocks)
         where = pl.ds(pl.multiple_of(b * take, 16), take)
-        to = flipped(me, o)
         return pltpu.make_async_remote_copy(
             src_ref=ready.at[slot, to],
             dst_ref=final.at[e, where, mine],
@@ -177,25 +186,31 @@
         def _():
             drain(k - QUEUE)
 
-        def one(s, carry):
-            line = 1.0 / jnp.sqrt(total[k, s])
-            for m in range(per):
-                d, where = place(s * per + m)
-                column = jnp.sum(jnp.where(shift == GROUP * m, line, 0.0), axis=1, keepdims=True)
-                x = norm_master[slot, d, where, :] + norm_second[slot, d, where, :].astype(jnp.float32)
-                ready[out, d, where, :] = (x * column).astype(jnp.bfloat16)
+        inverse[...] = 1.0 / jnp.sqrt(total[k])
+
+        def one(i, carry):
+            to = crossed(me, shards - 1 - i, bits)
+            for p in range(parts):
+                j = to * parts + p
+                where = pl.ds(p * GROUP, GROUP)
+                line = jnp.where(shift == GROUP * lax.rem(j, per), inverse[j // per], 0.0)
+                column = jnp.sum(line, axis=1, keepdims=True)
+                x = norm_master[slot, to, where, :] + norm_second[slot, to, where, :].astype(jnp.float32)
+                ready[out, to, where, :] = (x * column).astype(jnp.bfloat16)
+
+            @pl.when(i < shards - 1)
+            def _():
+                send(k, to).start()
+
             return carry
 
-        lax.fori_loop(0, lines, one, 0)
+        lax.fori_loop(0, shards, one, 0)
+        keep(k).start()
 
         @pl.when(k + READS < chunks)
         def _():
             for c in reads(k + READS, norm_bufs, norm_sems):
                 c.start()
-
-        for o in range(shards - 1, 0, -1):
-            send(k, o).start()
-        keep(k).start()
 
     first = min(DIRECT, chunks)
     row_sums(0, early.at[0, me])
@@ -217,7 +232,7 @@
             src_ref=rpart,
             dst_ref=rall.at[group, :, mine],
             send_sem=rsend,
-            recv_sem=rrecv.at[me],
+            recv_sem=rrecv,
             device_id={"shard": flipped(me, o)},
             device_id_type=MESH,
         )
@@ -238,9 +253,8 @@
 
         @pl.when((n >= 0) & (n < first))
         def _():
-            for o in range(1, shards):
-                other = flipped(me, o)
-                pltpu.make_async_copy(early.at[n, other], early.at[n, other], early_recv.at[n, other]).wait()
+            several = early.at[n, pl.ds(0, shards - 1)]
+            pltpu.make_async_copy(several, several, early_recv.at[n]).wait()
             sums = early[n, 0]
             for s in range(1, shards):
                 sums = sums + early[n, s]
@@ -275,17 +289,16 @@
         return pltpu.make_async_remote_copy(
             src_ref=rall.at[group],
             dst_ref=rall.at[group],
-            send_sem=gsend.at[o],
-            recv_sem=grecv.at[group],
+            send_sem=gsend,
+            recv_sem=grecv,
             device_id={"expert": lax.rem(group + o, groups)},
             device_id_type=MESH,
         )
 
     for o in range(1, shards):
         rows_copy(o).wait_send()
-        other = flipped(me, o)
-        there = rall.at[group, :, pl.ds(pl.multiple_of(other * cols, 128), cols)]
-        pltpu.make_async_copy(there, there, rrecv.at[other]).wait()
+    several = rall.at[group, :, pl.ds(0, (shards - 1) * cols)]
+    pltpu.make_async_copy(several, several, rrecv).wait()
     for o in range(1, groups):
         group_copy(o).start()
 
@@ -308,9 +321,9 @@
         scale[e : e + 1, :] = own[e, :, :rows]
 
     for o in range(1, groups):
-        other = lax.rem(group + o, groups)
-        pltpu.make_async_copy(rall.at[other], rall.at[other], grecv.at[other]).wait()
         group_copy(o).wait_send()
+    several = rall.at[pl.ds(0, groups - 1)]
+    pltpu.make_async_copy(several, several, grecv).wait()
     gcols = weight.shape[0]
     spot = lax.broadcasted_iota(jnp.int32, router.shape, 0)
     table = jnp.zeros(router.shape, jnp.float32)
@@ -401,19 +414,20 @@
             dma((QUEUE,)),
             dma((shards,)),
             dma((bits,)),
-            dma((bits, chunks)),
+            dma((bits, RING)),
             dma,
-            dma((chunks,)),
+            dma((RING,)),
             dma((first,)),
-            dma((first, shards)),
+            dma((first,)),
             dma,
-            dma((shards,)),
-            dma((groups,)),
-            dma((groups,)),
+            dma,
+            dma,
+            dma,
             pltpu.VMEM((gcols, cols), f32),
             pltpu.VMEM((1, cols), f32),
             dma((2,)),
             pltpu.VMEM((experts, 1, -(-rows // LANES) * LANES), f32),
+            pltpu.VMEM((lines, 1, LANES), f32),
         ],
         compiler_params=pltpu.CompilerParams(collective_id=0, has_side_effects=True, vmem_limit_bytes=28 * 2**20),
     )(

time: 307 us -> 305 us (level)
  no operation moved by 1% of the time
where the time goes in v2:
time: 305 us
  Pallas kernels  304 us (100%)
    pallas_call x1, Pallas kernels, local(): pl.pallas_call(functools.partial(kernel, shards, groups), out_shape=shape...  295 us
    pallas_call x1, Pallas kernels, local(): pl.pallas_call(write_out, out_shape=shapes, in_specs=[in_vmem] * 3, out_s...  8.99 us

profile of v2, /device:TPU:0, one launch (start us, length us, event | category | flops | bytes accessed | tf_op | source)
XLA Modules:
  0.0 304.8 jit_solution(7114021910989076956)
XLA Ops:
  0.6 295.2 %shard_map.67 = (bf16[4,800,4096]{2,1,0:T(8,128)(2,1)S(1)}, f32[4,800]{1,0:T(4,128)S(1)}, bf16[16,4096]{1,0:T(8,128)(2,1)S(1)}) custom-call(f32[4,8,800,512]{3,2,1,0:T(8,128)} %bitcast.5, bf16[4,8,800,512]{3,2,1,0:T(8,128)(2,1)} %bitcast.6, f32[4,512]{1,0:T(4,128)} %bitcast.7, f32[1,512]{1,0:T(1,128)} %bitcast.8), custom_call_target="tpu_custom_call" | custom-call | tf_op jit(solution)/shard_map/pallas_call | solution.py:394
  295.8 9.0 %shard_map.68 = (bf16[4,800,4096]{2,1,0:T(8,128)(2,1)}, f32[4,800]{1,0:T(4,128)}, bf16[16,4096]{1,0:T(8,128)(2,1)}) custom-call(bf16[4,800,4096]{2,1,0:T(8,128)(2,1)S(1)} %get-tuple-element.9.final, f32[4,800]{1,0:T(4,128)S(1)} %get-tuple-element.10.scale, bf16[16,4096]{1,0:T(8,128)(2,1)S(1)} %get-tuple-element.11.router), custom_call_target="tpu_custom_call" | custom-call | tf_op jit(solution)/shard_map/pallas_call | solution.py:439

commit v3 on v2

--- a/solution.py
+++ b/solution.py
@@ -46,7 +46,7 @@
     part, landed, total, early, rpart, rall,
     sum_sems, norm_sems, send_sems, own_sems, final_sems,
     part_send, part_recv, total_send, total_recv, early_send, early_recv,
-    rsend, rrecv, gsend, grecv, weight_here, gain_here, small_sems, own, inverse,
+    rsend, rrecv, gsend, grecv, weight_here, gain_here, small_sems, own, inverse, raw, raw_in, raw_send, raw_recv,
 ):
     experts, _, rows, cols = master.shape
     take = rows_per_chunk(rows)
@@ -99,7 +99,7 @@
         d, i = j // parts, lax.rem(j, parts)
         return d, pl.ds(pl.multiple_of(i * GROUP, GROUP), GROUP)
 
-    def row_sums(k, dst):
+    def row_sums(k, dst, copied=False):
         slot = lax.rem(k, READS)
         for c in reads(k, sum_bufs, sum_sems):
             c.wait()
@@ -115,6 +115,9 @@
             return carry
 
         lax.fori_loop(0, lines, one, 0)
+        if copied:
+            for d in range(shards):
+                raw[d] = sum_master[slot, d, :GROUP, :] + sum_second[slot, d, :GROUP, :].astype(jnp.float32)
 
         @pl.when(k + READS < chunks)
         def _():
@@ -131,6 +134,17 @@
             device_id_type=MESH,
         )
 
+    def raw_copy(o):
+        to = flipped(me, o)
+        return pltpu.make_async_remote_copy(
+            src_ref=raw.at[to],
+            dst_ref=raw_in.at[me],
+            send_sem=raw_send,
+            recv_sem=raw_recv,
+            device_id={"shard": to},
+            device_id_type=MESH,
+        )
+
     def exchange(stage, k):
         return pltpu.make_async_remote_copy(
             src_ref=part.at[stage, k],
@@ -159,7 +173,17 @@
             src_ref=ready.at[slot, to],
             dst_ref=final.at[e, where, mine],
             send_sem=send_sems.at[slot],
-            recv_sem=final_sems.at[me],
+            recv_sem=final_sems.at[e],
+            device_id={"shard": to},
+            device_id_type=MESH,
+        )
+
+    def send_rest(to):
+        return pltpu.make_async_remote_copy(
+            src_ref=ready.at[0, to, pl.ds(GROUP, take - GROUP)],
+            dst_ref=final.at[0, pl.ds(GROUP, take - GROUP), mine],
+            send_sem=send_sems.at[0],
+            recv_sem=final_sems.at[0],
             device_id={"shard": to},
             device_id_type=MESH,
         )
@@ -172,8 +196,18 @@
 
     def drain(k):
         slot = lax.rem(k, QUEUE)
-        several = ready.at[slot, pl.ds(0, shards - 1)]
-        pltpu.make_async_copy(several, several, send_sems.at[slot]).wait()
+
+
+        @pl.when(k > 0)
+        def _():
+            several = ready.at[slot, pl.ds(0, shards - 1)]
+            pltpu.make_async_copy(several, several, send_sems.at[slot]).wait()
+
+        @pl.when(k == 0)
+        def _():
+            several = ready.at[0, pl.ds(0, shards - 1), pl.ds(GROUP, take - GROUP)]
+            pltpu.make_async_copy(several, several, send_sems.at[0]).wait()
+
         keep(k).wait()
 
     def normalise(k):
@@ -198,10 +232,14 @@
                 x = norm_master[slot, to, where, :] + norm_second[slot, to, where, :].astype(jnp.float32)
                 ready[out, to, where, :] = (x * column).astype(jnp.bfloat16)
 
-            @pl.when(i < shards - 1)
+            @pl.when((i < shards - 1) & (k > 0))
             def _():
                 send(k, to).start()
 
+            @pl.when((i < shards - 1) & (k == 0))
+            def _():
+                send_rest(to).start()
+
             return carry
 
         lax.fori_loop(0, shards, one, 0)
@@ -213,13 +251,16 @@
                 c.start()
 
     first = min(DIRECT, chunks)
-    row_sums(0, early.at[0, me])
+    row_sums(0, early.at[0, me], copied=True)
     pl.semaphore_wait(barrier, shards + groups - 2)
     for k in range(first):
         if k:
             row_sums(k, early.at[k, me])
         for o in range(shards - 1, 0, -1):
             early_copy(k, o).start()
+        if k == 0:
+            for o in range(shards - 1, 0, -1):
+                raw_copy(o).start()
 
     for c in small:
         c.wait()
@@ -333,6 +374,18 @@
             table = jnp.where(spot == g * gcols + c, block[c : c + 1, :], table)
     router[...] = table.astype(jnp.bfloat16)
 
+    several = raw_in.at[pl.ds(0, shards - 1)]
+    pltpu.make_async_copy(several, several, raw_recv).wait()
+    pltpu.make_async_copy(several, several, raw_send).wait()
+    j = me * parts
+    line = jnp.where(shift == GROUP * lax.rem(j, per), 1.0 / jnp.sqrt(total[0, j // per]), 0.0)
+    column = jnp.sum(line, axis=1, keepdims=True)
+    for d in range(shards):
+
+        @pl.when(me != d)
+        def _():
+            final[0, :GROUP, d * cols : (d + 1) * cols] = (raw_in[d] * column).astype(jnp.bfloat16)
+
     for k in range(first):
         several = early.at[k, pl.ds(0, shards - 1)]
         pltpu.make_async_copy(several, several, early_send.at[k]).wait()
@@ -353,10 +406,10 @@
     lax.fori_loop(first, chunks, settle, 0)
     for k in range(max(0, chunks - QUEUE), chunks):
         drain(k)
-    for o in range(1, shards):
-        other = flipped(me, o)
-        there = final.at[:, :, pl.ds(pl.multiple_of(other * cols, 128), cols)]
-        pltpu.make_async_copy(there, there, final_sems.at[other]).wait()
+    for e in range(experts):
+        start = 0 if e else GROUP
+        there = final.at[e, pl.ds(start, rows - start), pl.ds(0, (shards - 1) * cols)]
+        pltpu.make_async_copy(there, there, final_sems.at[e]).wait()
 
 
 def write_out(final, scale, router, final_out, scale_out, router_out, sems):
@@ -412,7 +465,7 @@
             dma((2, READS)),
             dma((QUEUE,)),
             dma((QUEUE,)),
-            dma((shards,)),
+            dma((experts,)),
             dma((bits,)),
             dma((bits, RING)),
             dma,
@@ -428,6 +481,10 @@
             dma((2,)),
             pltpu.VMEM((experts, 1, -(-rows // LANES) * LANES), f32),
             pltpu.VMEM((lines, 1, LANES), f32),
+            pltpu.VMEM((shards, GROUP, cols), f32),
+            pltpu.VMEM((shards, GROUP, cols), f32),
+            dma,
+            dma,
         ],
         compiler_params=pltpu.CompilerParams(collective_id=0, has_side_effects=True, vmem_limit_bytes=28 * 2**20),
     )(

time: 305 us -> 304 us (level)
  no operation moved by 1% of the time
where the time goes in v3:
time: 304 us; the launch traced here: 303 us
  Pallas kernels  303 us (100%)
    pallas_call x1, Pallas kernels, local(): pl.pallas_call(functools.partial(kernel, shards, groups), out_shape=shape...  294 us
    pallas_call x1, Pallas kernels, local(): pl.pallas_call(write_out, out_shape=shapes, in_specs=[in_vmem] * 3, out_s...  8.99 us

profile of v3, /device:TPU:0, one launch (start us, length us, event | category | flops | bytes accessed | tf_op | source)
XLA Modules:
  0.0 303.4 jit_solution(13173395380164798110)
XLA Ops:
  0.6 293.8 %shard_map.67 = (bf16[4,800,4096]{2,1,0:T(8,128)(2,1)S(1)}, f32[4,800]{1,0:T(4,128)S(1)}, bf16[16,4096]{1,0:T(8,128)(2,1)S(1)}) custom-call(f32[4,8,800,512]{3,2,1,0:T(8,128)} %bitcast.5, bf16[4,8,800,512]{3,2,1,0:T(8,128)(2,1)} %bitcast.6, f32[4,512]{1,0:T(4,128)} %bitcast.7, f32[1,512]{1,0:T(1,128)} %bitcast.8), custom_call_target="tpu_custom_call" | custom-call | tf_op jit(solution)/shard_map/pallas_call | solution.py:447
  294.4 9.0 %shard_map.68 = (bf16[4,800,4096]{2,1,0:T(8,128)(2,1)}, f32[4,800]{1,0:T(4,128)}, bf16[16,4096]{1,0:T(8,128)(2,1)}) custom-call(bf16[4,800,4096]{2,1,0:T(8,128)(2,1)S(1)} %get-tuple-element.9.final, f32[4,800]{1,0:T(4,128)S(1)} %get-tuple-element.10.scale, bf16[16,4096]{1,0:T(8,128)(2,1)S(1)} %get-tuple-element.11.router), custom_call_target="tpu_custom_call" | custom-call | tf_op jit(solution)/shard_map/pallas_call | solution.py:496
